TPU v7x, 512 devices: a whole 4x8x8 slice. The times are simulated.
512 devices in a mesh: section: 4 (over y_hi), dp: 128 (over z, x, y_lo, core).
Axes of the slice: x: 4, y: 8 (y_hi: 4, y_lo: 2; y = y_hi * 2 + y_lo), z: 8, core: 2. Of those that a mesh axis runs over, the one named last changes fastest.
Arguments:
- saved_inputs: bfloat16 [4, 2, 16384, 320], P('section', None, 'dp'), may hold values from -6 to 6
- timesteps: int32 [2, 16384], P(None, 'dp'), may hold values from 0 to 999
- time_table: bfloat16 [1000, 320], replicated, may hold values from -6 to 6
- skip_weight: bfloat16 [4, 320, 320], P('section'), may hold values from -0.3125 to 0.3125
- ff_in: bfloat16 [4, 1280, 320], P('section'), may hold values from -0.3125 to 0.3125
- ff_out: bfloat16 [4, 1280, 320], P('section'), may hold values from -0.15625 to 0.15625
- output_cotangent: bfloat16 [2, 16384, 320], P(None, 'dp'), may hold values from -6 to 6
Outputs:
- input_grads: bfloat16 [4, 2, 16384, 320], P('section', None, 'dp')
- skip_weight_grad: float32 [4, 102400], P('section', 'dp')
- ff_in_grad: float32 [4, 1280, 320], P('section', 'dp')
- ff_out_grad: float32 [4, 1280, 320], P('section', 'dp')
All inputs are finite; a program needn't handle non-finite values.
Results may differ from a plain program's by a relative error of at most 0.01.
Values may be sent and summed in bfloat16 or wider, within the bound.
A program may use at most 128 MiB of HBM per device.

v0:
```python
import jax
import jax.numpy as jnp
from jax import lax
from jax.experimental import pallas as pl
from jax.experimental.pallas import tpu as pltpu
from jax.sharding import Mesh
from jax.sharding import PartitionSpec as P

DP = ("z", "x", "w", "core")
MESH = pl.DeviceIdType.MESH
EPS = 1e-06
CHUNKS = 8
LAG = 4
FF_ROWS = 40
BLOCK = 48
PIECE = 16
F32 = jnp.float32
BF16 = jnp.bfloat16


def dot(left, right):
    return jnp.dot(left, right, preferred_element_type=F32)


def dot_nt(left, right):
    return lax.dot_general(left, right, (((1,), (1,)), ((), ())), preferred_element_type=F32)


def kernel(
    xt_hbm,
    ts_hbm,
    tablet_hbm,
    wskip_hbm,
    wint_hbm,
    woutt_hbm,
    cott_hbm,
    grads_ref,
    din_ref,
    dout_ref,
    dskip_ref,
    xt_ref,
    ts_ref,
    tablet_ref,
    wskip_ref,
    wint_ref,
    woutt_ref,
    cott_ref,
    in_sem,
    ga_buf,
    v_msg,
    g_msg,
    k_msg,
    x_buf,
    z_buf,
    g_buf,
    vsend,
    csend,
    ksend,
    u_buf,
    r_buf,
    ds_buf,
    ch_buf,
    chsh_buf,
    nq,
    gq,
    sel,
    win_q,
    wout_q,
    act_t,
    ds_q,
    gpre_t,
    za_t,
    zb_t,
    skip_part,
    skip_core,
    skip_w,
    part,
    r_x1,
    r_x2,
    z_send,
    r_z,
    vs_sem,
    vr_sem,
    cs_sem,
    cr_sem,
    ks_sem,
    kr_sem,
    n_s,
    n_r,
    gs_s,
    gs_r,
    sk_s,
    sk_r,
    x1_s,
    x1_r,
    x1k_s,
    x1k_r,
    x2_s,
    x2_r,
    z_s,
    z_r,
):
    section = lax.axis_index("section")
    mz = lax.axis_index("z")
    mx = lax.axis_index("x")
    mw = lax.axis_index("w")
    mc = lax.axis_index("core")
    pairs = (
        (ts_hbm, ts_ref),
        (tablet_hbm, tablet_ref),
        (xt_hbm, xt_ref),
        (wskip_hbm, wskip_ref),
        (wint_hbm, wint_ref),
        (woutt_hbm, woutt_ref),
        (cott_hbm, cott_ref),
    )
    loads = [pltpu.make_async_copy(a, b, in_sem.at[i]) for i, (a, b) in enumerate(pairs)]
    for load in loads:
        load.start()
    micro, width, per = xt_ref.shape
    total = micro * per
    rows = total // CHUNKS
    levels = tablet_ref.shape[1]
    hidden = wint_ref.shape[1]

    def remote(src, dst, send, recv, device):
        return pltpu.make_async_remote_copy(
            src_ref=src,
            dst_ref=dst,
            send_sem=send,
            recv_sem=recv,
            device_id=device,
            device_id_type=MESH,
        )

    x_near = mx + 1 - 2 * lax.rem(mx, 2)
    x_far = 3 - mx
    x_op = lax.rem(mx + 2, 4)

    barrier = pltpu.get_barrier_semaphore()
    greet = [{"section": lax.rem(section + step, 4)} for step in (1, 3)]
    greet += [{"core": 1 - mc}, {"x": x_near}, {"x": x_far}, {"w": 1 - mw}]
    greet += [{"z": lax.rem(mz + step, 8)} for step in range(1, 8)]
    for device in greet:
        pl.semaphore_signal(barrier, inc=1, device_id=device, device_id_type=MESH)
    pl.semaphore_wait(barrier, len(greet))

    def at(c):
        return pl.ds(pl.multiple_of(c * rows, rows), rows)

    def value_copy(c):
        device = {"section": 3 - section}
        return remote(vsend.at[c], v_msg.at[c], vs_sem.at[c], vr_sem.at[c], device)

    def chain_copy(c):
        device = {"section": lax.rem(section + 3, 4)}
        return remote(csend.at[c], g_msg.at[c], cs_sem.at[c], cr_sem.at[c], device)

    def skip_copy(c):
        device = {"section": lax.rem(section + 1, 4)}
        return remote(ksend.at[c], k_msg.at[c], ks_sem.at[c], kr_sem.at[c], device)

    def paced(copy, c):
        @pl.when(c >= 2)
        def _():
            copy(c - 2).wait_send()

        copy(c).start()

    rest = width - 256
    short = rows // 2

    def pack(buf, c, value):
        value = value.astype(BF16)
        buf[c, 0:rows, :] = value[:, 0:128]
        buf[c, rows : 2 * rows, :] = value[:, 128:256]
        buf[c, 2 * rows :, 0:rest] = value[0:short, 256:width]
        buf[c, 2 * rows :, rest:] = value[short:, 256:width]

    def unpack(buf, c):
        tail = jnp.concatenate([buf[c, 2 * rows :, 0:rest], buf[c, 2 * rows :, rest:]], axis=0)
        return jnp.concatenate([buf[c, 0:rows, :], buf[c, rows : 2 * rows, :], tail], axis=1)

    def forward(c, kind):
        here = at(c)
        if kind == "decoder":
            value_copy(c).wait_recv()
            z_buf[here, :] = unpack(v_msg, c)
        united = x_buf[here, :] + dot(z_buf[here, :], wskip_ref[...])
        recip = lax.rsqrt(jnp.mean(united * united, axis=-1, keepdims=True) + EPS)
        normed = (united * recip).astype(BF16)
        preact = dot(normed, wint_ref[...])
        sigma = jax.nn.sigmoid(preact)
        active = (preact * sigma).astype(BF16)
        if kind == "encoder":
            pack(vsend, c, united + dot_nt(active, woutt_ref[...]))
            paced(value_copy, c)
        u_buf[here, :] = united
        r_buf[here, :] = jnp.broadcast_to(recip, (rows, 128))
        nq[me, here, 0:width] = normed
        ds_buf[here, :] = sigma * (1.0 + preact * (1.0 - sigma))

    def finish(c, gy, low, gact):
        here = at(c)
        pre = (gact * ds_buf[here, :]).astype(BF16)
        gn = dot_nt(pre, wint_ref[...])
        united = u_buf[here, :]
        recip = r_buf[here, 0:1]
        mean = jnp.mean(gn * united, axis=-1, keepdims=True)
        chain = gy + recip * gn - united * (recip * recip * recip * mean)
        low_chain = chain.astype(BF16)
        ch_buf[here, 0:width] = low_chain
        chsh_buf[here, 64 : 64 + width] = low_chain
        return low_chain

    def backward(c, which):
        here = at(c)
        if which == 3:
            low = g_buf[here, :]
            chain = finish(c, low.astype(F32), low, ga_buf[here, :])
            pack(csend, c, chain)
            paced(chain_copy, c)
            pack(ksend, c, dot_nt(chain, wskip_ref[...]))
            paced(skip_copy, c)
            return
        chain_copy(c).wait_recv()
        gy = unpack(g_msg, c).astype(F32)
        if which == 0:
            skip_copy(c).wait_recv()
            gy = gy + unpack(k_msg, c).astype(F32)
        low = gy.astype(BF16)
        gq[me, here, 64 : 64 + width] = low
        if which == 0:
            for to in range(2):
                share_g(c, to).start()
        chain = finish(c, gy, low, dot(low, woutt_ref[...]))
        if which == 2:
            back = dot_nt(chain, wskip_ref[...]).astype(BF16)
            pack(csend, c, chain.astype(F32) + back.astype(F32))
        if which == 1:
            pack(csend, c, chain)
        if which > 0:
            paced(chain_copy, c)

    me = 2 * mw + mc
    mates = (2 * mw + 1 - mc, 2 * (1 - mw) + mc, 2 * (1 - mw) + 1 - mc)
    towards = ({"core": 1 - mc}, {"w": 1 - mw}, {"core": 1 - mc})

    def share_n(to):
        slot = mates[1] if to == 2 else me
        return remote(nq.at[slot], nq.at[slot], n_s.at[to], n_r.at[to], towards[to])

    def share_g(c, to):
        slot = mates[1] if to == 2 else me
        block = gq.at[slot, at(c)]
        return remote(block, block, gs_s.at[to, c], gs_r.at[to, c], towards[to])

    nq[me, :, width:] = jnp.zeros((total, 384 - width), BF16)
    gq[me, :, 0:64] = jnp.zeros((total, 64), BF16)
    ch_buf[:, width:] = jnp.zeros((total, 384 - width), BF16)
    chsh_buf[:, 0:64] = jnp.zeros((total, 64), BF16)

    def rows_of(m):
        return slice(m * per, (m + 1) * per)

    @pl.when(section < 2)
    def _():
        for load in loads[0:2]:
            load.wait()
        for m in range(micro):
            onehot = ts_ref[m : m + 1, :] == lax.broadcasted_iota(jnp.int32, (levels, per), 0)
            embed = dot(tablet_ref[...], jnp.where(onehot, 1.0, 0.0).astype(BF16))
            z_buf[rows_of(m), :] = embed.T.astype(BF16)

    loads[2].wait()
    for m in range(micro):
        x_buf[rows_of(m), :] = xt_ref[m].astype(F32).T
    for load in loads[3:]:
        load.wait()

    @pl.when(section < 2)
    def _():
        @pl.loop(0, CHUNKS)
        def _(c):
            forward(c, "encoder")

    @pl.when(section >= 2)
    def _():
        for load in loads[0:2]:
            load.wait()

    @pl.when(section == 3)
    def _():
        for m in range(micro):
            cot = cott_ref[m].astype(F32).T.astype(BF16)
            g_buf[rows_of(m), :] = cot
            gq[me, rows_of(m), 64 : 64 + width] = cot
        ga_buf[...] = dot(g_buf[...], woutt_ref[...])

        @pl.loop(0, CHUNKS)
        def _(c):
            forward(c, "decoder")
            backward(c, 3)

    @pl.when(section == 2)
    def _():
        @pl.loop(0, CHUNKS + LAG)
        def _(t):
            @pl.when(t < CHUNKS)
            def _():
                forward(t, "decoder")

            @pl.when(t >= LAG)
            def _():
                backward(t - LAG, 2)

    for to in range(2):
        share_n(to).start()
    line = lax.broadcasted_iota(jnp.int32, (hidden, width), 1)
    unit = 40 * (4 * (lax.rem(line, 80) // 10) + line // 80) + 10 * me + lax.rem(line, 10)
    chosen = lax.broadcasted_iota(jnp.int32, (hidden, width), 0) == unit
    sel[...] = jnp.where(chosen, 1.0, 0.0).astype(BF16)
    win_q[...] = dot(wint_ref[...], sel[...]).astype(BF16)
    wout_q[0:64, :] = jnp.zeros((64, width), BF16)
    wout_q[64:, :] = dot(woutt_ref[...], sel[...]).astype(BF16)
    slot = lax.broadcasted_iota(jnp.int32, (256, width), 0)
    channel = lax.broadcasted_iota(jnp.int32, (256, width), 1)
    third = lax.rem(slot, 2)
    pixel = lax.rem(slot, 64) // 2
    first = 10 * (4 * lax.rem(pixel, 8) + pixel // 8) + 5 * lax.rem(slot // 64, 2)
    first = first + 2 * (slot // 128)
    for dst, pick in (
        (za_t, channel == first + 2 * third),
        (zb_t, (channel == first + 1) & (third == 0)),
    ):
        dst[...] = dot_nt(jnp.where(pick, 1.0, 0.0).astype(BF16), z_buf[...]).astype(BF16)
    share_n(1).wait_recv()
    share_n(2).start()
    share_n(0).wait_recv()
    share_n(2).wait_recv()

    @pl.loop(0, 4)
    def _(q):
        preact = dot(nq[q, :, 0:width], win_q[...])
        sigma = jax.nn.sigmoid(preact)
        ds_q[q] = sigma * (1.0 + preact * (1.0 - sigma))
        act_t[:, pl.ds(pl.multiple_of(q * total, total), total)] = (preact * sigma).astype(BF16).T

    for which in (0, 1):

        @pl.when(section == which)
        def _():
            @pl.loop(0, CHUNKS)
            def _(c):
                backward(c, which)

    def joined(left, right):
        return left[:, 0:256], left[:, 256:384] + right[:, 0:128], right[:, 128:384]

    edges = (slice(0, 256), slice(256, 384), slice(384, 640))

    @pl.when(section > 0)
    def _():
        @pl.loop(0, CHUNKS)
        def _(c):
            for to in range(2):
                share_g(c, to).start()

    skips = joined(dot(za_t[...], ch_buf[...]), dot(zb_t[...], chsh_buf[...]))
    for edge, value in zip(edges, skips):
        skip_part[:, :, :, edge] = value.astype(BF16).reshape(2, 2, 64, -1)
    skip1 = remote(skip_part.at[1 - mc], skip_core, sk_s.at[0], sk_r.at[0], {"core": 1 - mc})
    skip2 = remote(skip_part.at[mc, 1 - mw], skip_w, sk_s.at[1], sk_r.at[1], {"w": 1 - mw})
    skip1.start()

    @pl.loop(0, CHUNKS)
    def _(c):
        share_g(c, 1).wait_recv()
        share_g(c, 2).start()

    skip1.wait_recv()
    other = skip_part[mc, 1 - mw].astype(F32) + skip_core[1 - mw].astype(F32)
    skip_part[mc, 1 - mw] = other.astype(BF16)
    skip2.start()
    own_skip = skip_part[mc, mw].astype(F32) + skip_core[mw].astype(F32)
    skip_part[mc, mw] = own_skip.astype(BF16)

    def through(q):
        pre = (dot(gq[q], wout_q[...]) * ds_q[q]).astype(BF16)
        gpre_t[:, pl.ds(pl.multiple_of(q * total, total), total)] = pre.T

    through(me)
    through(mates[1])
    for to in (0, 2):

        @pl.loop(0, CHUNKS)
        def _(c):
            share_g(c, to).wait_recv()

        through(mates[to])

    everyone = 4 * total
    d_out = dot(act_t[...], gq[...].reshape(everyone, 384))
    d_in = dot(gpre_t[...], nq[...].reshape(everyone, 384))
    for edge, value in zip(edges, joined(d_in, d_out)):
        value = value.astype(BF16).reshape(4, 2, FF_ROWS, -1)
        for color in range(2):
            part[color, :, 0:FF_ROWS, edge] = value[:, color]

    def x1_block(color, k):
        device = x_far if color else x_near
        return device, device if k == 0 else x_op

    def x1_copy(color, k):
        device, block = x1_block(color, k)
        span = pl.ds(0, FF_ROWS)
        src, dst = part.at[color, block, span], r_x1.at[color, k, span]
        return remote(src, dst, x1_s.at[color, k], x1_r.at[color, k], {"x": device})

    def x1k_copy(color, k):
        device, block = x1_block(color, k)
        span = pl.ds(FF_ROWS, BLOCK - FF_ROWS)
        src, dst = part.at[color, block, span], r_x1.at[color, k, span]
        return remote(src, dst, x1k_s.at[color, k], x1k_r.at[color, k], {"x": device})

    def x2_copy(color):
        device = x_near if color else x_far
        src = part.at[color, device]
        return remote(src, r_x2.at[color], x2_s.at[color], x2_r.at[color], {"x": device})

    for k in (1, 0):
        for color in range(2):
            x1_copy(color, k).start()
    skip2.wait_recv()
    own = (skip_part[mc, mw].astype(F32) + skip_w[...].astype(F32)).astype(BF16)
    own = own.reshape(4, 2, BLOCK - FF_ROWS, 2 * width)
    for color in range(2):
        part[color, :, FF_ROWS:, :] = own[:, color]
    for k in (1, 0):
        for color in range(2):
            x1k_copy(color, k).start()
    for m in range(micro):
        grads_ref[m] = ch_buf[m * per : (m + 1) * per, 0:width].astype(F32).T.astype(BF16)

    def added(left, right):
        return left.astype(F32) + right.astype(F32)

    for color in range(2):
        other = x_near if color else x_far
        for k in (1, 0):
            x1_copy(color, k).wait_recv()
            x1k_copy(color, k).wait_recv()
            block = other if k == 1 else mx
            part[color, block] = added(part[color, block], r_x1[color, k]).astype(BF16)
            if k == 1:
                x2_copy(color).start()

    def z_copy(k):
        target = lax.rem(mz + k, 8)
        return remote(z_send.at[target], r_z.at[mz], z_s.at[k], z_r.at[mz], {"z": target})

    for color in range(2):
        x2_copy(color).wait_recv()
        block = added(part[color, mx], r_x2[color])
        for j in range(4):
            piece = (
                block[10 * j : 10 * j + 10],
                block[FF_ROWS + 2 * j : FF_ROWS + 2 * j + 2],
                jnp.zeros((PIECE - 12, 2 * width), F32),
            )
            z_send[4 * color + j] = jnp.concatenate(piece, axis=0).astype(BF16)
    far_first = (4, 3, 5, 2, 6, 1, 7)
    for k in far_first:
        z_copy(k).start()
    acc = z_send[mz].astype(F32)
    for k in reversed(far_first):
        source = lax.rem(mz + 8 - k, 8)
        slot = r_z.at[source]
        remote(slot, slot, z_s.at[k], z_r.at[source], {"z": source}).wait_recv()
        acc = acc + r_z[source].astype(F32)

    for j in range(10):
        din_ref[j] = acc[j : j + 1, 0:width]
        dout_ref[j] = acc[j : j + 1, width:]
    half = width // 2
    lead, mid, last = acc[10:11, 0:width], acc[10:11, width:], acc[11:12, 0:width]

    @pl.when(mc == 0)
    def _():
        dskip_ref[:, 0:width] = lead
        dskip_ref[:, width : 2 * width] = mid
        dskip_ref[:, 2 * width :] = last[:, 0:half]

    @pl.when(mc == 1)
    def _():
        dskip_ref[:, 0:half] = lead[:, half:]
        dskip_ref[:, half : half + width] = mid
        dskip_ref[:, half + width :] = last

    for to in range(3):
        share_n(to).wait_send()
    skip1.wait_send()
    skip2.wait_send()

    @pl.loop(0, CHUNKS)
    def _(c):
        for to in range(3):
            share_g(c, to).wait_send()

    @pl.when(section < 2)
    def _():
        for late in range(1, 3):
            value_copy(CHUNKS - late).wait_send()

    @pl.when(section > 0)
    def _():
        for late in range(1, 3):
            chain_copy(CHUNKS - late).wait_send()

    @pl.when(section == 3)
    def _():
        for late in range(1, 3):
            skip_copy(CHUNKS - late).wait_send()

    for color in range(2):
        for k in range(2):
            x1_copy(color, k).wait_send()
            x1k_copy(color, k).wait_send()
        x2_copy(color).wait_send()
    for k in range(1, 8):
        z_copy(k).wait_send()


def finish(*refs):
    copies = [pltpu.make_async_copy(refs[i], refs[4 + i], refs[8].at[i]) for i in range(4)]
    for copy in copies:
        copy.start()
    for copy in copies:
        copy.wait()


def shards(saved_inputs, timesteps, time_table, skip_weight, ff_in, ff_out, output_cotangent):
    n_micro, per, width = saved_inputs.shape[1:]
    hidden = ff_in.shape[1]
    total = n_micro * per
    lanes = 2 * width
    shapes = (
        jax.ShapeDtypeStruct((n_micro, width, per), BF16),
        jax.ShapeDtypeStruct((10, 1, width), F32),
        jax.ShapeDtypeStruct((10, 1, width), F32),
        jax.ShapeDtypeStruct((1, 800), F32),
    )
    low = pltpu.VMEM((total, width), BF16)
    message = pltpu.VMEM((CHUNKS, total // CHUNKS * width // 128, 128), BF16)
    wide = pltpu.VMEM((total, 384), BF16)
    dma = pltpu.SemaphoreType.DMA
    held = pl.pallas_call(
        kernel,
        out_shape=tuple(pltpu.VMEM(s.shape, s.dtype) for s in shapes),
        in_specs=[pl.BlockSpec(memory_space=pl.ANY)] * 7,
        out_specs=(pl.BlockSpec(memory_space=pltpu.VMEM),) * 4,
        scratch_shapes=[
            pltpu.VMEM((n_micro, width, per), BF16),
            pltpu.VMEM(timesteps.shape, jnp.int32),
            pltpu.VMEM((width, time_table.shape[0]), BF16),
            pltpu.VMEM((width, width), BF16),
            pltpu.VMEM((width, hidden), BF16),
            pltpu.VMEM((width, hidden), BF16),
            pltpu.VMEM((n_micro, width, per), BF16),
            dma((7,)),
            pltpu.VMEM((total, hidden), F32),
            message,
            message,
            message,
            pltpu.VMEM((total, width), F32),
            low,
            low,
            message,
            message,
            message,
            pltpu.VMEM((total, width), F32),
            pltpu.VMEM((total, 128), F32),
            pltpu.VMEM((total, hidden), F32),
            wide,
            wide,
            pltpu.VMEM((4, total, 384), BF16),
            pltpu.VMEM((4, total, 384), BF16),
            pltpu.VMEM((hidden, width), BF16),
            pltpu.VMEM((width, width), BF16),
            pltpu.VMEM((384, width), BF16),
            pltpu.VMEM((width, 4 * total), BF16),
            pltpu.VMEM((4, total, width), F32),
            pltpu.VMEM((width, 4 * total), BF16),
            pltpu.VMEM((256, total), BF16),
            pltpu.VMEM((256, total), BF16),
            pltpu.VMEM((2, 2, 64, lanes), BF16),
            pltpu.VMEM((2, 64, lanes), BF16),
            pltpu.VMEM((64, lanes), BF16),
            pltpu.VMEM((2, 4, BLOCK, lanes), BF16),
            pltpu.VMEM((2, 2, BLOCK, lanes), BF16),
            pltpu.VMEM((2, BLOCK, lanes), BF16),
            pltpu.VMEM((8, PIECE, lanes), BF16),
            pltpu.VMEM((8, PIECE, lanes), BF16),
        ]
        + [dma((CHUNKS,))] * 6
        + [dma((3,))] * 2
        + [dma((3, CHUNKS))] * 2
        + [dma((2,))] * 2
        + [dma((2, 2))] * 4
        + [dma((2,))] * 2
        + [dma((8,))] * 2,
        compiler_params=pltpu.CompilerParams(collective_id=0, has_side_effects=True),
    )(
        jnp.swapaxes(saved_inputs[0], 1, 2),
        timesteps,
        time_table.T,
        skip_weight[0],
        ff_in[0].T,
        ff_out[0].T,
        jnp.swapaxes(output_cotangent, 1, 2),
    )
    grads, d_in, d_out, d_skip = pl.pallas_call(
        finish,
        out_shape=shapes,
        in_specs=[pl.BlockSpec(memory_space=pltpu.VMEM)] * 4,
        out_specs=(pl.BlockSpec(memory_space=pl.ANY),) * 4,
        scratch_shapes=[dma((4,))],
        compiler_params=pltpu.CompilerParams(vmem_limit_bytes=2**20),
    )(*held)
    grads = jnp.swapaxes(grads, 1, 2)[None]
    return (grads, d_skip, jnp.swapaxes(d_in, 0, 1), jnp.swapaxes(d_out, 0, 1))


def solution(mesh):
    split = Mesh(
        mesh.devices.reshape(mesh.shape["section"], 8, 4, 2, 2), ("section", "z", "x", "w", "core")
    )
    return jax.shard_map(
        shards,
        mesh=split,
        in_specs=(
            P("section", None, DP, None),
            P(None, DP),
            P(),
            P("section", None, None),
            P("section", None, None),
            P("section", None, None),
            P(None, DP, None),
        ),
        out_specs=(
            P("section", None, DP, None),
            P("section", DP),
            P("section", DP, None),
            P("section", DP, None),
        ),
        check_vma=False,
    )
```

profile of v0, /device:TPU:1, one launch (start us, length us, event | category | flops | bytes accessed | tf_op | source)
XLA Modules:
  0.0 62.3 jit_solution(5074532242842326952)
XLA Ops:
  0.6 61.0 %shard_map.102 = (bf16[2,320,128]{2,1,0:T(8,128)(2,1)S(1)}, f32[10,1,320]{2,1,0:T(1,128)S(1)}, f32[10,1,320]{2,1,0:T(1,128)S(1)}, f32[1,800]{1,0:T(1,128)S(1)}) custom-call(bf16[2,320,128]{2,1,0:T(8,128)(2,1)} %bitcast.21, s32[2,128]{1,0:T(2,128)} %ts_hbm.1, bf16[320,1000]{1,0:T(8,128)(2,1)} %bitcast.19, bf16[320,320]{1,0:T(8,128)(2,1)} %bitcast.20, ...), custom_call_target="tpu_custom_call" | custom-call | tf_op jit(solution)/shard_map/pallas_call | solution.py:557
  61.6 0.7 %shard_map.103 = (bf16[2,320,128]{2,1,0:T(8,128)(2,1)}, f32[10,1,320]{2,1,0:T(1,128)}, f32[10,1,320]{2,1,0:T(1,128)}, f32[1,800]{1,0:T(1,128)}) custom-call(bf16[2,320,128]{2,1,0:T(8,128)(2,1)S(1)} %get-tuple-element.12.refs_0_, f32[10,1,320]{2,1,0:T(1,128)S(1)} %get-tuple-element.13.refs_1_, f32[10,1,320]{2,1,0:T(1,128)S(1)} %get-tuple-element.14.refs_2_, ...), custom_call_target="tpu_custom_call" | custom-call | tf_op jit(solution)/shard_map/pallas_call | solution.py:622
where the time goes:
time: 63.3 us; the launch traced here: 62.3 us
  Pallas kernels  61.7 us (97%)
  between operations  0.64 us (1%)
    pallas_call x1, Pallas kernels, shards(): pl.pallas_call(kernel, out_shape=tuple((pltpu.VMEM(s.shape, s.dtype) for...  61 us

commit v1 on v0

--- a/solution.py
+++ b/solution.py
@@ -9,10 +9,9 @@
 DP = ("z", "x", "w", "core")
 MESH = pl.DeviceIdType.MESH
 EPS = 1e-06
-CHUNKS = 8
-LAG = 4
+CHUNKS = 4
+LAG = 3
 FF_ROWS = 40
-BLOCK = 48
 PIECE = 16
 F32 = jnp.float32
 BF16 = jnp.bfloat16
@@ -66,6 +65,8 @@
     sel,
     win_q,
     wout_q,
+    win_n,
+    wout_n,
     act_t,
     ds_q,
     gpre_t,
@@ -73,10 +74,11 @@
     zb_t,
     skip_part,
     skip_core,
-    skip_w,
     part,
     r_x1,
     r_x2,
+    own_skip,
+    r_own,
     z_send,
     r_z,
     vs_sem,
@@ -89,12 +91,13 @@
     n_r,
     gs_s,
     gs_r,
+    gw_r,
     sk_s,
     sk_r,
     x1_s,
     x1_r,
-    x1k_s,
-    x1k_r,
+    own_s,
+    own_r,
     x2_s,
     x2_r,
     z_s,
@@ -139,13 +142,15 @@
 
     barrier = pltpu.get_barrier_semaphore()
     greet = [{"section": lax.rem(section + step, 4)} for step in (1, 3)]
-    greet += [{"core": 1 - mc}, {"x": x_near}, {"x": x_far}, {"w": 1 - mw}]
+    greet += [{"core": 1 - mc}, {"x": x_near}, {"x": x_far}, {"x": x_op}, {"w": 1 - mw}]
+    greet += [{"w": 1 - mw, "x": to} for to in (x_near, x_far, x_op)]
     greet += [{"z": lax.rem(mz + step, 8)} for step in range(1, 8)]
     for device in greet:
         pl.semaphore_signal(barrier, inc=1, device_id=device, device_id_type=MESH)
-    pl.semaphore_wait(barrier, len(greet))
 
     def at(c):
+        if isinstance(c, int):
+            return slice(c * rows, (c + 1) * rows)
         return pl.ds(pl.multiple_of(c * rows, rows), rows)
 
     def value_copy(c):
@@ -181,49 +186,49 @@
         tail = jnp.concatenate([buf[c, 2 * rows :, 0:rest], buf[c, 2 * rows :, rest:]], axis=0)
         return jnp.concatenate([buf[c, 0:rows, :], buf[c, rows : 2 * rows, :], tail], axis=1)
 
-    def forward(c, kind):
-        here = at(c)
-        if kind == "decoder":
-            value_copy(c).wait_recv()
-            z_buf[here, :] = unpack(v_msg, c)
-        united = x_buf[here, :] + dot(z_buf[here, :], wskip_ref[...])
+    def front(c, z):
+        united = x_buf[at(c), :] + dot(z, wskip_ref[...])
         recip = lax.rsqrt(jnp.mean(united * united, axis=-1, keepdims=True) + EPS)
         normed = (united * recip).astype(BF16)
         preact = dot(normed, wint_ref[...])
         sigma = jax.nn.sigmoid(preact)
-        active = (preact * sigma).astype(BF16)
-        if kind == "encoder":
-            pack(vsend, c, united + dot_nt(active, woutt_ref[...]))
-            paced(value_copy, c)
+        return united, recip, normed, preact, sigma, sigma * (1.0 + preact * (1.0 - sigma))
+
+    def keep(c, united, recip, normed, slope):
+        here = at(c)
         u_buf[here, :] = united
         r_buf[here, :] = jnp.broadcast_to(recip, (rows, 128))
         nq[me, here, 0:width] = normed
-        ds_buf[here, :] = sigma * (1.0 + preact * (1.0 - sigma))
-
-    def finish(c, gy, low, gact):
-        here = at(c)
-        pre = (gact * ds_buf[here, :]).astype(BF16)
-        gn = dot_nt(pre, wint_ref[...])
-        united = u_buf[here, :]
-        recip = r_buf[here, 0:1]
+        ds_buf[here, :] = slope
+
+    def encode(c):
+        united, recip, normed, preact, sigma, slope = front(c, z_buf[at(c), :])
+        active = (preact * sigma).astype(BF16)
+        pack(vsend, c, united + dot(active, wout_n[...]))
+        paced(value_copy, c)
+        keep(c, united, recip, normed, slope)
+
+    def back(gy, gact, united, recip, slope):
+        pre = (gact * slope).astype(BF16)
+        gn = dot(pre, win_n[...])
         mean = jnp.mean(gn * united, axis=-1, keepdims=True)
         chain = gy + recip * gn - united * (recip * recip * recip * mean)
-        low_chain = chain.astype(BF16)
-        ch_buf[here, 0:width] = low_chain
-        chsh_buf[here, 64 : 64 + width] = low_chain
-        return low_chain
+        return chain.astype(BF16)
+
+    def keep_chain(c, chain):
+        here = at(c)
+        ch_buf[here, 0:width] = chain
+        chsh_buf[here, 64 : 64 + width] = chain
 
     def backward(c, which):
         here = at(c)
-        if which == 3:
-            low = g_buf[here, :]
-            chain = finish(c, low.astype(F32), low, ga_buf[here, :])
-            pack(csend, c, chain)
-            paced(chain_copy, c)
-            pack(ksend, c, dot_nt(chain, wskip_ref[...]))
-            paced(skip_copy, c)
-            return
         chain_copy(c).wait_recv()
+        if which == 1:
+
+            @pl.when(c >= 2)
+            def _():
+                chain_copy(c - 2).wait_send()
+
         gy = unpack(g_msg, c).astype(F32)
         if which == 0:
             skip_copy(c).wait_recv()
@@ -231,16 +236,52 @@
         low = gy.astype(BF16)
         gq[me, here, 64 : 64 + width] = low
         if which == 0:
-            for to in range(2):
-                share_g(c, to).start()
-        chain = finish(c, gy, low, dot(low, woutt_ref[...]))
-        if which == 2:
-            back = dot_nt(chain, wskip_ref[...]).astype(BF16)
-            pack(csend, c, chain.astype(F32) + back.astype(F32))
+            share(c)
+        gact = dot(low, woutt_ref[...])
+        chain = back(gy, gact, u_buf[here, :], r_buf[here, 0:1], ds_buf[here, :])
         if which == 1:
             pack(csend, c, chain)
-        if which > 0:
-            paced(chain_copy, c)
+            chain_copy(c).start()
+        keep_chain(c, chain)
+
+    def when(condition, action):
+        pl.when(condition)(action)
+
+    def step2_front(f):
+        value_copy(f).wait_recv()
+        z = unpack(v_msg, f)
+        united, recip, normed, _, _, slope = front(f, z)
+        z_buf[at(f), :] = z
+        keep(f, united, recip, normed, slope)
+
+    def step2_back(b):
+        chain_copy(b).wait_recv()
+        when(b >= 2, lambda: chain_copy(b - 2).wait_send())
+        here = at(b)
+        low = unpack(g_msg, b)
+        gact = dot(low, woutt_ref[...])
+        chain = back(low.astype(F32), gact, u_buf[here, :], r_buf[here, 0:1], ds_buf[here, :])
+        joint = chain.astype(F32) + dot_nt(chain, wskip_ref[...]).astype(BF16).astype(F32)
+        pack(csend, b, joint)
+        chain_copy(b).start()
+        gq[me, here, 64 : 64 + width] = low
+        keep_chain(b, chain)
+
+    def step3(c):
+        here = at(c)
+        value_copy(c).wait_recv()
+        when(c >= 2, lambda: chain_copy(c - 2).wait_send())
+        when(c >= 2, lambda: skip_copy(c - 2).wait_send())
+        z = unpack(v_msg, c)
+        united, recip, normed, _, _, slope = front(c, z)
+        chain = back(g_buf[here, :].astype(F32), ga_buf[here, :], united, recip, slope)
+        pack(csend, c, chain)
+        chain_copy(c).start()
+        pack(ksend, c, dot_nt(chain, wskip_ref[...]))
+        skip_copy(c).start()
+        z_buf[here, :] = z
+        nq[me, here, 0:width] = normed
+        keep_chain(c, chain)
 
     me = 2 * mw + mc
     mates = (2 * mw + 1 - mc, 2 * (1 - mw) + mc, 2 * (1 - mw) + 1 - mc)
@@ -253,7 +294,20 @@
     def share_g(c, to):
         slot = mates[1] if to == 2 else me
         block = gq.at[slot, at(c)]
-        return remote(block, block, gs_s.at[to, c], gs_r.at[to, c], towards[to])
+        got = gw_r.at[c] if to == 1 else gs_r.at[to]
+        return remote(block, block, gs_s.at[to], got, towards[to])
+
+    def whole_g(to):
+        block = gq.at[me if to < 2 else mates[1]]
+        return remote(block, block, gs_s.at[to], gs_r.at[to], towards[to])
+
+    def share(c):
+        for to in range(2):
+            share_g(c, to).start()
+
+    def share_normed():
+        for to in range(2):
+            share_n(to).start()
 
     nq[me, :, width:] = jnp.zeros((total, 384 - width), BF16)
     gq[me, :, 0:64] = jnp.zeros((total, 64), BF16)
@@ -263,31 +317,32 @@
     def rows_of(m):
         return slice(m * per, (m + 1) * per)
 
+    def choose_units():
+        line = lax.broadcasted_iota(jnp.int32, (hidden, width), 1)
+        unit = 40 * (4 * (lax.rem(line, 80) // 10) + line // 80) + 10 * me + lax.rem(line, 10)
+        chosen = lax.broadcasted_iota(jnp.int32, (hidden, width), 0) == unit
+        sel[...] = jnp.where(chosen, 1.0, 0.0).astype(BF16)
+        win_q[...] = dot(wint_ref[...], sel[...]).astype(BF16)
+        wout_q[0:64, :] = jnp.zeros((64, width), BF16)
+        wout_q[64:, :] = dot(woutt_ref[...], sel[...]).astype(BF16)
+
+    def embed(m):
+        onehot = ts_ref[m : m + 1, :] == lax.broadcasted_iota(jnp.int32, (levels, per), 0)
+        rows_t = dot(tablet_ref[...], jnp.where(onehot, 1.0, 0.0).astype(BF16))
+        z_buf[rows_of(m), :] = rows_t.T.astype(BF16)
+
+    for load in loads[0:3]:
+        load.wait()
+
     @pl.when(section < 2)
     def _():
-        for load in loads[0:2]:
-            load.wait()
         for m in range(micro):
-            onehot = ts_ref[m : m + 1, :] == lax.broadcasted_iota(jnp.int32, (levels, per), 0)
-            embed = dot(tablet_ref[...], jnp.where(onehot, 1.0, 0.0).astype(BF16))
-            z_buf[rows_of(m), :] = embed.T.astype(BF16)
-
-    loads[2].wait()
+            embed(m)
+
     for m in range(micro):
         x_buf[rows_of(m), :] = xt_ref[m].astype(F32).T
     for load in loads[3:]:
         load.wait()
-
-    @pl.when(section < 2)
-    def _():
-        @pl.loop(0, CHUNKS)
-        def _(c):
-            forward(c, "encoder")
-
-    @pl.when(section >= 2)
-    def _():
-        for load in loads[0:2]:
-            load.wait()
 
     @pl.when(section == 3)
     def _():
@@ -297,32 +352,58 @@
             gq[me, rows_of(m), 64 : 64 + width] = cot
         ga_buf[...] = dot(g_buf[...], woutt_ref[...])
 
+    @pl.when(section < 2)
+    def _():
+        wout_n[...] = woutt_ref[...].T
+
+    @pl.when(section >= 2)
+    def _():
+        win_n[...] = wint_ref[...].T
+
+    pl.semaphore_wait(barrier, len(greet))
+
+    @pl.when(section < 2)
+    def _():
         @pl.loop(0, CHUNKS)
         def _(c):
-            forward(c, "decoder")
-            backward(c, 3)
+            encode(c)
+
+        share_normed()
+        win_n[...] = wint_ref[...].T
+        choose_units()
+
+    @pl.when(section == 3)
+    def _():
+        @pl.loop(0, CHUNKS)
+        def _(c):
+            share(c)
+
+        choose_units()
+
+        @pl.loop(0, CHUNKS)
+        def _(c):
+            step3(c)
+
+        share_normed()
 
     @pl.when(section == 2)
     def _():
-        @pl.loop(0, CHUNKS + LAG)
+        choose_units()
+
+        @pl.loop(0, LAG)
         def _(t):
-            @pl.when(t < CHUNKS)
+            step2_front(t)
+
+        @pl.loop(0, CHUNKS)
+        def _(t):
+            step2_back(t)
+
+            @pl.when(t < CHUNKS - LAG)
             def _():
-                forward(t, "decoder")
-
-            @pl.when(t >= LAG)
-            def _():
-                backward(t - LAG, 2)
-
-    for to in range(2):
-        share_n(to).start()
-    line = lax.broadcasted_iota(jnp.int32, (hidden, width), 1)
-    unit = 40 * (4 * (lax.rem(line, 80) // 10) + line // 80) + 10 * me + lax.rem(line, 10)
-    chosen = lax.broadcasted_iota(jnp.int32, (hidden, width), 0) == unit
-    sel[...] = jnp.where(chosen, 1.0, 0.0).astype(BF16)
-    win_q[...] = dot(wint_ref[...], sel[...]).astype(BF16)
-    wout_q[0:64, :] = jnp.zeros((64, width), BF16)
-    wout_q[64:, :] = dot(woutt_ref[...], sel[...]).astype(BF16)
+                step2_front(t + LAG)
+
+        share_normed()
+
     slot = lax.broadcasted_iota(jnp.int32, (256, width), 0)
     channel = lax.broadcasted_iota(jnp.int32, (256, width), 1)
     third = lax.rem(slot, 2)
@@ -334,6 +415,7 @@
         (zb_t, (channel == first + 1) & (third == 0)),
     ):
         dst[...] = dot_nt(jnp.where(pick, 1.0, 0.0).astype(BF16), z_buf[...]).astype(BF16)
+
     share_n(1).wait_recv()
     share_n(2).start()
     share_n(0).wait_recv()
@@ -359,19 +441,23 @@
 
     edges = (slice(0, 256), slice(256, 384), slice(384, 640))
 
-    @pl.when(section > 0)
+    @pl.when((section == 1) | (section == 2))
     def _():
         @pl.loop(0, CHUNKS)
         def _(c):
-            for to in range(2):
-                share_g(c, to).start()
+            share(c)
 
     skips = joined(dot(za_t[...], ch_buf[...]), dot(zb_t[...], chsh_buf[...]))
     for edge, value in zip(edges, skips):
         skip_part[:, :, :, edge] = value.astype(BF16).reshape(2, 2, 64, -1)
     skip1 = remote(skip_part.at[1 - mc], skip_core, sk_s.at[0], sk_r.at[0], {"core": 1 - mc})
-    skip2 = remote(skip_part.at[mc, 1 - mw], skip_w, sk_s.at[1], sk_r.at[1], {"w": 1 - mw})
     skip1.start()
+
+    def own_copy(k):
+        v = 1 - mw if k % 2 else mw
+        to = (mx, x_near, x_far, x_op)[k // 2]
+        return remote(own_skip.at[v, to], r_own.at[k - 1], own_s.at[0], own_r.at[0], {"w": v, "x": to})
+
 
     @pl.loop(0, CHUNKS)
     def _(c):
@@ -379,12 +465,9 @@
         share_g(c, 2).start()
 
     skip1.wait_recv()
-    other = skip_part[mc, 1 - mw].astype(F32) + skip_core[1 - mw].astype(F32)
-    skip_part[mc, 1 - mw] = other.astype(BF16)
-    skip2.start()
-    own_skip = skip_part[mc, mw].astype(F32) + skip_core[mw].astype(F32)
-    skip_part[mc, mw] = own_skip.astype(BF16)
-
+    for v in range(2):
+        mine = skip_part[mc, v].astype(F32) + skip_core[v].astype(F32)
+        own_skip[v] = mine.astype(BF16).reshape(4, PIECE, 2 * width)
     def through(q):
         pre = (dot(gq[q], wout_q[...]) * ds_q[q]).astype(BF16)
         gpre_t[:, pl.ds(pl.multiple_of(q * total, total), total)] = pre.T
@@ -392,11 +475,7 @@
     through(me)
     through(mates[1])
     for to in (0, 2):
-
-        @pl.loop(0, CHUNKS)
-        def _(c):
-            share_g(c, to).wait_recv()
-
+        whole_g(to).wait_recv()
         through(mates[to])
 
     everyone = 4 * total
@@ -405,23 +484,13 @@
     for edge, value in zip(edges, joined(d_in, d_out)):
         value = value.astype(BF16).reshape(4, 2, FF_ROWS, -1)
         for color in range(2):
-            part[color, :, 0:FF_ROWS, edge] = value[:, color]
-
-    def x1_block(color, k):
+            part[color, :, :, edge] = value[:, color]
+
+    def x1_copy(color, k):
         device = x_far if color else x_near
-        return device, device if k == 0 else x_op
-
-    def x1_copy(color, k):
-        device, block = x1_block(color, k)
-        span = pl.ds(0, FF_ROWS)
-        src, dst = part.at[color, block, span], r_x1.at[color, k, span]
+        block = device if k == 0 else x_op
+        src, dst = part.at[color, block], r_x1.at[color, k]
         return remote(src, dst, x1_s.at[color, k], x1_r.at[color, k], {"x": device})
-
-    def x1k_copy(color, k):
-        device, block = x1_block(color, k)
-        span = pl.ds(FF_ROWS, BLOCK - FF_ROWS)
-        src, dst = part.at[color, block, span], r_x1.at[color, k, span]
-        return remote(src, dst, x1k_s.at[color, k], x1k_r.at[color, k], {"x": device})
 
     def x2_copy(color):
         device = x_near if color else x_far
@@ -431,53 +500,71 @@
     for k in (1, 0):
         for color in range(2):
             x1_copy(color, k).start()
-    skip2.wait_recv()
-    own = (skip_part[mc, mw].astype(F32) + skip_w[...].astype(F32)).astype(BF16)
-    own = own.reshape(4, 2, BLOCK - FF_ROWS, 2 * width)
-    for color in range(2):
-        part[color, :, FF_ROWS:, :] = own[:, color]
+    for k in range(7, 0, -1):
+        own_copy(k).start()
+    for m in range(micro):
+        grads_ref[m] = ch_buf[m * per : (m + 1) * per, 0:width].astype(F32).T.astype(BF16)
+
+    def added(left, right):
+        return left.astype(F32) + right.astype(F32)
+
     for k in (1, 0):
         for color in range(2):
-            x1k_copy(color, k).start()
-    for m in range(micro):
-        grads_ref[m] = ch_buf[m * per : (m + 1) * per, 0:width].astype(F32).T.astype(BF16)
-
-    def added(left, right):
-        return left.astype(F32) + right.astype(F32)
-
-    for color in range(2):
-        other = x_near if color else x_far
-        for k in (1, 0):
             x1_copy(color, k).wait_recv()
-            x1k_copy(color, k).wait_recv()
-            block = other if k == 1 else mx
+            block = mx if k == 0 else (x_near if color else x_far)
             part[color, block] = added(part[color, block], r_x1[color, k]).astype(BF16)
             if k == 1:
                 x2_copy(color).start()
 
     def z_copy(k):
         target = lax.rem(mz + k, 8)
-        return remote(z_send.at[target], r_z.at[mz], z_s.at[k], z_r.at[mz], {"z": target})
-
+        return remote(z_send.at[target], r_z.at[k - 1], z_s.at[0], z_r.at[0], {"z": target})
+
+    for to in range(3):
+        share_n(to).wait_send()
+    skip1.wait_send()
+
+    for to in range(3):
+        whole_g(to).wait_send()
+
+    @pl.when(section < 2)
+    def _():
+        for late in range(1, 3):
+            value_copy(CHUNKS - late).wait_send()
+
+    @pl.when(section > 0)
+    def _():
+        for late in range(1, 3):
+            chain_copy(CHUNKS - late).wait_send()
+
+    @pl.when(section == 3)
+    def _():
+        for late in range(1, 3):
+            skip_copy(CHUNKS - late).wait_send()
+
+    tails = own_skip[mw, mx].astype(F32)
+    all_own = remote(r_own, r_own, own_s.at[0], own_r.at[0], {"w": 1 - mw})
+    all_own.wait_recv()
+    for k in range(7):
+        tails = tails + r_own[k].astype(F32)
     for color in range(2):
         x2_copy(color).wait_recv()
         block = added(part[color, mx], r_x2[color])
         for j in range(4):
-            piece = (
-                block[10 * j : 10 * j + 10],
-                block[FF_ROWS + 2 * j : FF_ROWS + 2 * j + 2],
-                jnp.zeros((PIECE - 12, 2 * width), F32),
-            )
-            z_send[4 * color + j] = jnp.concatenate(piece, axis=0).astype(BF16)
+            piece = (block[10 * j : 10 * j + 10], tails[8 * color + 2 * j : 8 * color + 2 * j + 2])
+            piece = jnp.concatenate(piece, axis=0)
+            stack = [piece[:, 128 * t : 128 * t + 128] for t in range(5)]
+            stack = jnp.concatenate(stack + [jnp.zeros((4, 128), F32)], axis=0)
+            z_send[4 * color + j] = stack.astype(BF16)
     far_first = (4, 3, 5, 2, 6, 1, 7)
     for k in far_first:
         z_copy(k).start()
     acc = z_send[mz].astype(F32)
-    for k in reversed(far_first):
-        source = lax.rem(mz + 8 - k, 8)
-        slot = r_z.at[source]
-        remote(slot, slot, z_s.at[k], z_r.at[source], {"z": source}).wait_recv()
-        acc = acc + r_z[source].astype(F32)
+    all_z = remote(r_z, r_z, z_s.at[0], z_r.at[0], {"z": lax.rem(mz + 1, 8)})
+    all_z.wait_recv()
+    for k in range(7):
+        acc = acc + r_z[k].astype(F32)
+    acc = jnp.concatenate([acc[12 * t : 12 * t + 12] for t in range(5)], axis=1)
 
     for j in range(10):
         din_ref[j] = acc[j : j + 1, 0:width]
@@ -497,38 +584,12 @@
         dskip_ref[:, half : half + width] = mid
         dskip_ref[:, half + width :] = last
 
-    for to in range(3):
-        share_n(to).wait_send()
-    skip1.wait_send()
-    skip2.wait_send()
-
-    @pl.loop(0, CHUNKS)
-    def _(c):
-        for to in range(3):
-            share_g(c, to).wait_send()
-
-    @pl.when(section < 2)
-    def _():
-        for late in range(1, 3):
-            value_copy(CHUNKS - late).wait_send()
-
-    @pl.when(section > 0)
-    def _():
-        for late in range(1, 3):
-            chain_copy(CHUNKS - late).wait_send()
-
-    @pl.when(section == 3)
-    def _():
-        for late in range(1, 3):
-            skip_copy(CHUNKS - late).wait_send()
-
     for color in range(2):
         for k in range(2):
             x1_copy(color, k).wait_send()
-            x1k_copy(color, k).wait_send()
         x2_copy(color).wait_send()
-    for k in range(1, 8):
-        z_copy(k).wait_send()
+    all_own.wait_send()
+    all_z.wait_send()
 
 
 def finish(*refs):
@@ -588,6 +649,8 @@
             pltpu.VMEM((hidden, width), BF16),
             pltpu.VMEM((width, width), BF16),
             pltpu.VMEM((384, width), BF16),
+            pltpu.VMEM((hidden, width), BF16),
+            pltpu.VMEM((hidden, width), BF16),
             pltpu.VMEM((width, 4 * total), BF16),
             pltpu.VMEM((4, total, width), F32),
             pltpu.VMEM((width, 4 * total), BF16),
@@ -595,20 +658,23 @@
             pltpu.VMEM((256, total), BF16),
             pltpu.VMEM((2, 2, 64, lanes), BF16),
             pltpu.VMEM((2, 64, lanes), BF16),
-            pltpu.VMEM((64, lanes), BF16),
-            pltpu.VMEM((2, 4, BLOCK, lanes), BF16),
-            pltpu.VMEM((2, 2, BLOCK, lanes), BF16),
-            pltpu.VMEM((2, BLOCK, lanes), BF16),
-            pltpu.VMEM((8, PIECE, lanes), BF16),
-            pltpu.VMEM((8, PIECE, lanes), BF16),
+            pltpu.VMEM((2, 4, FF_ROWS, lanes), BF16),
+            pltpu.VMEM((2, 2, FF_ROWS, lanes), BF16),
+            pltpu.VMEM((2, FF_ROWS, lanes), BF16),
+            pltpu.VMEM((2, 4, PIECE, lanes), BF16),
+            pltpu.VMEM((7, PIECE, lanes), BF16),
+            pltpu.VMEM((8, 64, 128), BF16),
+            pltpu.VMEM((7, 64, 128), BF16),
         ]
         + [dma((CHUNKS,))] * 6
         + [dma((3,))] * 2
-        + [dma((3, CHUNKS))] * 2
+        + [dma((3,))] * 2
+        + [dma((CHUNKS,))]
+        + [dma((1,))] * 2
+        + [dma((2, 2))] * 2
+        + [dma((1,))] * 2
         + [dma((2,))] * 2
-        + [dma((2, 2))] * 4
-        + [dma((2,))] * 2
-        + [dma((8,))] * 2,
+        + [dma((1,))] * 2,
         compiler_params=pltpu.CompilerParams(collective_id=0, has_side_effects=True),
     )(
         jnp.swapaxes(saved_inputs[0], 1, 2),

time: 63.3 us -> 62.9 us (level); the launches traced: 62.3 us -> 62.7 us
  no operation moved by 1% of the time
where the time goes in v1:
time: 62.9 us; the launch traced here: 62.7 us
  Pallas kernels  62.1 us (99%)
  between operations  0.64 us (1%)
    pallas_call x1, Pallas kernels, shards(): pl.pallas_call(kernel, out_shape=tuple((pltpu.VMEM(s.shape, s.dtype) for...  61.4 us

profile of v1, /device:TPU:1, one launch (start us, length us, event | category | flops | bytes accessed | tf_op | source)
XLA Modules:
  0.0 62.7 jit_solution(16250728516372947154)
XLA Ops:
  0.6 61.4 %shard_map.102 = (bf16[2,320,128]{2,1,0:T(8,128)(2,1)S(1)}, f32[10,1,320]{2,1,0:T(1,128)S(1)}, f32[10,1,320]{2,1,0:T(1,128)S(1)}, f32[1,800]{1,0:T(1,128)S(1)}) custom-call(bf16[2,320,128]{2,1,0:T(8,128)(2,1)} %bitcast.21, s32[2,128]{1,0:T(2,128)} %ts_hbm.1, bf16[320,1000]{1,0:T(8,128)(2,1)} %bitcast.19, bf16[320,320]{1,0:T(8,128)(2,1)} %bitcast.20, ...), custom_call_target="tpu_custom_call" | custom-call | tf_op jit(solution)/shard_map/pallas_call | solution.py:618
  62.0 0.7 %shard_map.103 = (bf16[2,320,128]{2,1,0:T(8,128)(2,1)}, f32[10,1,320]{2,1,0:T(1,128)}, f32[10,1,320]{2,1,0:T(1,128)}, f32[1,800]{1,0:T(1,128)}) custom-call(bf16[2,320,128]{2,1,0:T(8,128)(2,1)S(1)} %get-tuple-element.12.refs_0_, f32[10,1,320]{2,1,0:T(1,128)S(1)} %get-tuple-element.13.refs_1_, f32[10,1,320]{2,1,0:T(1,128)S(1)} %get-tuple-element.14.refs_2_, ...), custom_call_target="tpu_custom_call" | custom-call | tf_op jit(solution)/shard_map/pallas_call | solution.py:688

commit v2 on v1

--- a/solution.py
+++ b/solution.py
@@ -9,8 +9,8 @@
 DP = ("z", "x", "w", "core")
 MESH = pl.DeviceIdType.MESH
 EPS = 1e-06
-CHUNKS = 4
-LAG = 3
+CHUNKS = 8
+LAG = 5
 FF_ROWS = 40
 PIECE = 16
 F32 = jnp.float32
@@ -225,9 +225,9 @@
         chain_copy(c).wait_recv()
         if which == 1:
 
-            @pl.when(c >= 2)
+            @pl.when(c >= 3)
             def _():
-                chain_copy(c - 2).wait_send()
+                chain_copy(c - 3).wait_send()
 
         gy = unpack(g_msg, c).astype(F32)
         if which == 0:
@@ -256,7 +256,7 @@
 
     def step2_back(b):
         chain_copy(b).wait_recv()
-        when(b >= 2, lambda: chain_copy(b - 2).wait_send())
+        when(b >= 3, lambda: chain_copy(b - 3).wait_send())
         here = at(b)
         low = unpack(g_msg, b)
         gact = dot(low, woutt_ref[...])
@@ -270,7 +270,7 @@
     def step3(c):
         here = at(c)
         value_copy(c).wait_recv()
-        when(c >= 2, lambda: chain_copy(c - 2).wait_send())
+        when(c >= 3, lambda: chain_copy(c - 3).wait_send())
         when(c >= 2, lambda: skip_copy(c - 2).wait_send())
         z = unpack(v_msg, c)
         united, recip, normed, _, _, slope = front(c, z)
@@ -534,7 +534,7 @@
 
     @pl.when(section > 0)
     def _():
-        for late in range(1, 3):
+        for late in range(1, 4):
             chain_copy(CHUNKS - late).wait_send()
 
     @pl.when(section == 3)

time: 62.9 us -> 60.8 us (0.967)
  Pallas kernels: 62.1 us -> 60 us
    pallas_call x1, Pallas kernels: 61.4 us -> 59.3 us  [shards(): pl.pallas_call(kernel, out_shape=tuple((pltpu.VMEM(s.shape, s.dtype) for...]
where the time goes in v2:
time: 60.8 us; the launch traced here: 60.6 us
  Pallas kernels  60 us (99%)
  between operations  0.64 us (1%)
    pallas_call x1, Pallas kernels, shards(): pl.pallas_call(kernel, out_shape=tuple((pltpu.VMEM(s.shape, s.dtype) for...  59.3 us

profile of v2, /device:TPU:1, one launch (start us, length us, event | category | flops | bytes accessed | tf_op | source)
XLA Modules:
  0.0 60.6 jit_solution(4789994057722747767)
XLA Ops:
  0.6 59.3 %shard_map.102 = (bf16[2,320,128]{2,1,0:T(8,128)(2,1)S(1)}, f32[10,1,320]{2,1,0:T(1,128)S(1)}, f32[10,1,320]{2,1,0:T(1,128)S(1)}, f32[1,800]{1,0:T(1,128)S(1)}) custom-call(bf16[2,320,128]{2,1,0:T(8,128)(2,1)} %bitcast.21, s32[2,128]{1,0:T(2,128)} %ts_hbm.1, bf16[320,1000]{1,0:T(8,128)(2,1)} %bitcast.19, bf16[320,320]{1,0:T(8,128)(2,1)} %bitcast.20, ...), custom_call_target="tpu_custom_call" | custom-call | tf_op jit(solution)/shard_map/pallas_call | solution.py:618
  59.9 0.7 %shard_map.103 = (bf16[2,320,128]{2,1,0:T(8,128)(2,1)}, f32[10,1,320]{2,1,0:T(1,128)}, f32[10,1,320]{2,1,0:T(1,128)}, f32[1,800]{1,0:T(1,128)}) custom-call(bf16[2,320,128]{2,1,0:T(8,128)(2,1)S(1)} %get-tuple-element.12.refs_0_, f32[10,1,320]{2,1,0:T(1,128)S(1)} %get-tuple-element.13.refs_1_, f32[10,1,320]{2,1,0:T(1,128)S(1)} %get-tuple-element.14.refs_2_, ...), custom_call_target="tpu_custom_call" | custom-call | tf_op jit(solution)/shard_map/pallas_call | solution.py:688

commit v3 on v2

--- a/solution.py
+++ b/solution.py
@@ -459,24 +459,28 @@
         return remote(own_skip.at[v, to], r_own.at[k - 1], own_s.at[0], own_r.at[0], {"w": v, "x": to})
 
 
-    @pl.loop(0, CHUNKS)
-    def _(c):
-        share_g(c, 1).wait_recv()
-        share_g(c, 2).start()
-
+    def through(q):
+        pre = (dot(gq[q], wout_q[...]) * ds_q[q]).astype(BF16)
+        gpre_t[:, pl.ds(pl.multiple_of(q * total, total), total)] = pre.T
+
+    def pass_on():
+        @pl.loop(0, CHUNKS)
+        def _(c):
+            share_g(c, 1).wait_recv()
+            share_g(c, 2).start()
+
+    when(mw == 0, pass_on)
+    through(me)
+    whole_g(0).wait_recv()
+    through(mates[0])
+    when(mw == 1, pass_on)
     skip1.wait_recv()
     for v in range(2):
         mine = skip_part[mc, v].astype(F32) + skip_core[v].astype(F32)
         own_skip[v] = mine.astype(BF16).reshape(4, PIECE, 2 * width)
-    def through(q):
-        pre = (dot(gq[q], wout_q[...]) * ds_q[q]).astype(BF16)
-        gpre_t[:, pl.ds(pl.multiple_of(q * total, total), total)] = pre.T
-
-    through(me)
     through(mates[1])
-    for to in (0, 2):
-        whole_g(to).wait_recv()
-        through(mates[to])
+    whole_g(2).wait_recv()
+    through(mates[2])
 
     everyone = 4 * total
     d_out = dot(act_t[...], gq[...].reshape(everyone, 384))

time: 60.8 us -> 60.8 us (level)
  no operation moved by 1% of the time
where the time goes in v3:
time: 60.8 us; the launch traced here: 60.6 us
  Pallas kernels  60 us (99%)
  between operations  0.64 us (1%)
    pallas_call x1, Pallas kernels, shards(): pl.pallas_call(kernel, out_shape=tuple((pltpu.VMEM(s.shape, s.dtype) for...  59.3 us

profile of v3, /device:TPU:1, one launch (start us, length us, event | category | flops | bytes accessed | tf_op | source)
XLA Modules:
  0.0 60.6 jit_solution(8018562241016715646)
XLA Ops:
  0.6 59.3 %shard_map.102 = (bf16[2,320,128]{2,1,0:T(8,128)(2,1)S(1)}, f32[10,1,320]{2,1,0:T(1,128)S(1)}, f32[10,1,320]{2,1,0:T(1,128)S(1)}, f32[1,800]{1,0:T(1,128)S(1)}) custom-call(bf16[2,320,128]{2,1,0:T(8,128)(2,1)} %bitcast.21, s32[2,128]{1,0:T(2,128)} %ts_hbm.1, bf16[320,1000]{1,0:T(8,128)(2,1)} %bitcast.19, bf16[320,320]{1,0:T(8,128)(2,1)} %bitcast.20, ...), custom_call_target="tpu_custom_call" | custom-call | tf_op jit(solution)/shard_map/pallas_call | solution.py:622
  59.9 0.7 %shard_map.103 = (bf16[2,320,128]{2,1,0:T(8,128)(2,1)}, f32[10,1,320]{2,1,0:T(1,128)}, f32[10,1,320]{2,1,0:T(1,128)}, f32[1,800]{1,0:T(1,128)}) custom-call(bf16[2,320,128]{2,1,0:T(8,128)(2,1)S(1)} %get-tuple-element.12.refs_0_, f32[10,1,320]{2,1,0:T(1,128)S(1)} %get-tuple-element.13.refs_1_, f32[10,1,320]{2,1,0:T(1,128)S(1)} %get-tuple-element.14.refs_2_, ...), custom_call_target="tpu_custom_call" | custom-call | tf_op jit(solution)/shard_map/pallas_call | solution.py:692
